TPU v7x, 32 devices: a whole 2x2x4 slice. The times are simulated.
32 devices in a mesh: child: 4 (over z), rows: 8 (over y, x, core).
Axes of the slice: x: 2, y: 2, z: 4, core: 2. Of those that a mesh axis runs over, the one named last changes fastest.
Arguments:
- omega: bfloat16 [4, 8192, 512], P('child', 'rows'), may hold values from -6 to 6
- leaf_diag: bfloat16 [4, 32, 256, 256], P('child', 'rows'), may hold values from -0.375 to 0.375
- leaf_u: bfloat16 [4, 8192, 128], P('child', 'rows'), may hold values from -0.5 to 0.5
- leaf_v: bfloat16 [4, 8192, 128], P('child', 'rows'), may hold values from -0.375 to 0.375
- coupling: bfloat16 [4, 4096, 4096], P('child', 'rows'), may hold values from -0.09375 to 0.09375
- child_map: int32 [4, 64], P('child', 'rows'), may hold values from 0 to 95, as said below
Outputs:
- parent_rows: float32 [3, 4096, 512], P(None, ('child', 'rows'))
Inputs may be any that keep to these rules, and one draw needn't show every extreme that they name: `child_map`: child block b of every child maps to one of the parent blocks 3 * (b // 2), 3 * (b // 2) + 1, 3 * (b // 2) + 2, and blocks 2 k and 2 k + 1 map to two different ones of their triple, the lower first.
All inputs are finite; a program needn't handle non-finite values.
Results may differ from a plain program's by a relative error of at most 0.004.
Values may be sent and summed in bfloat16 or wider, within the bound.
A program may use at most 128 MiB of HBM per device.

v0:
```python
import functools

import jax
import jax.numpy as jnp
from jax import lax
from jax.experimental import pallas as pl
from jax.experimental.pallas import tpu as pltpu
from jax.sharding import PartitionSpec as P

MESH = pl.DeviceIdType.MESH
WIDTH = 128
DEPTH = 4096
STEPS = 2


def dot(a, b):
    return jnp.dot(a, b, preferred_element_type=jnp.float32)


def kernel(
    n_child, n_rows, omega_hbm, v_hbm, map_ref, diag_hbm, u_hbm, coupling_hbm, arrived, slots_in,
    omega, v, diag, u, coupling, gathered, local_part, total, coupled, update, slots,
    load_sem, ici_send, ici_recv, fwd_send, fwd_recv, core_send, core_recv,
    z_send, z_recv, map_send, map_recv, keep_sem,
):
    chunks = gathered.shape[0]
    leaves, leaf = diag.shape[0], diag.shape[1]
    rank = u.shape[1]
    block = leaves * rank
    chips = n_rows // 2
    c = lax.axis_index("child")
    r = lax.axis_index("rows")
    chip, core = r // 2, r % 2
    partner = chip * 2 + 1 - core

    forward = chips == 4
    if forward:
        x, y = chip % 2, chip // 2
        x_near = (y * 2 + 1 - x) * 2
        y_near = ((1 - y) * 2 + x) * 2
        first = x_near * (1 - core) + y_near * core
        second = y_near * (1 - core) + x_near * core
        across = ((1 - y) * 2 + 1 - x) * 2
        direct = [(second + core, second + core), (first + core, first + core)]
        other = [first + 1 - core, second + 1 - core]
    else:
        direct = [
            (((chip + d) % chips) * 2 + core, ((chip + chips - d) % chips) * 2 + core)
            for d in range(1, chips)
        ]
        other = [((chip + chips - d) % chips) * 2 + 1 - core for d in range(1, chips)]
    sources = [r] + [s for _, s in direct]
    other = [partner] + other
    if forward:
        sources.append(across + core)
        other.append(across + 1 - core)
    if n_child == 4:
        peers = [((c + 2) % 4,) * 2, (3 - c,) * 2, (c + 1 - 2 * (c % 2),) * 2]
    else:
        peers = [((c + d) % n_child, (c + n_child - d) % n_child) for d in range(1, n_child)]

    barrier = pltpu.get_barrier_semaphore()
    for to, _ in direct + [(partner, partner)]:
        pl.semaphore_signal(barrier, inc=1, device_id=(c, to), device_id_type=MESH)
    for to, _ in peers:
        pl.semaphore_signal(barrier, inc=1, device_id=(to, r), device_id_type=MESH)

    loads = [
        pltpu.make_async_copy(v_hbm.at[0], v, load_sem.at[0]),
        pltpu.make_async_copy(
            omega_hbm.at[0, :, :WIDTH], omega.at[:, :WIDTH], load_sem.at[1]
        ),
        pltpu.make_async_copy(
            omega_hbm.at[0, :, WIDTH:], omega.at[:, WIDTH:], load_sem.at[2]
        ),
        pltpu.make_async_copy(coupling_hbm.at[0], coupling, load_sem.at[3]),
        pltpu.make_async_copy(diag_hbm.at[0], diag, load_sem.at[4]),
        pltpu.make_async_copy(u_hbm.at[0], u, load_sem.at[5]),
    ]
    for load in loads:
        load.start()

    def rows_of(k, source):
        return gathered.at[k, pl.ds(pl.multiple_of(source * block, block), block)]

    def project(first, last):
        for i in range(leaves):
            rows = slice(i * leaf, (i + 1) * leaf)
            projected = lax.dot_general(
                v[rows, :],
                omega[rows, first * WIDTH : last * WIDTH],
                (((0,), (0,)), ((), ())),
                preferred_element_type=jnp.float32,
            ).astype(jnp.bfloat16)
            at = pl.ds(pl.multiple_of(r * block + i * rank, rank), rank)
            for k in range(first, last):
                gathered[k, at, :] = projected[:, (k - first) * WIDTH : (k - first + 1) * WIDTH]

    for i in range(leaves):
        for b in range(2):
            slot = map_ref[0, 2 * i + b] - 3 * (r * leaves + i)
            slots[i, 4 * b : 4 * b + 4, :] = jnp.full(
                (4, slots.shape[2]), slot, jnp.int32
            ).astype(jnp.float32)

    def ici(t, k):
        return pltpu.make_async_remote_copy(
            src_ref=rows_of(k, r), dst_ref=rows_of(k, r), send_sem=ici_send.at[t, k],
            recv_sem=ici_recv.at[t, k], device_id=(c, direct[t][0]), device_id_type=MESH,
        )

    def ici_in(t, k):
        at = rows_of(k, direct[t][1])
        return pltpu.make_async_remote_copy(
            src_ref=at, dst_ref=at, send_sem=ici_send.at[t, k],
            recv_sem=ici_recv.at[t, k], device_id=(c, direct[t][0]), device_id_type=MESH,
        )

    def fwd(k):
        at = rows_of(k, direct[0][1])
        return pltpu.make_async_remote_copy(
            src_ref=at, dst_ref=at, send_sem=fwd_send.at[k],
            recv_sem=fwd_recv.at[k], device_id=(c, direct[1][0]), device_id_type=MESH,
        )

    def fwd_in(k):
        at = rows_of(k, sources[-1])
        return pltpu.make_async_remote_copy(
            src_ref=at, dst_ref=at, send_sem=fwd_send.at[k],
            recv_sem=fwd_recv.at[k], device_id=(c, direct[1][0]), device_id_type=MESH,
        )

    def across_core(t, k, who):
        at = rows_of(k, who[t])
        return pltpu.make_async_remote_copy(
            src_ref=at, dst_ref=at, send_sem=core_send.at[t, k],
            recv_sem=core_recv.at[t, k], device_id=(c, partner), device_id_type=MESH,
        )

    def to_peer(j, k):
        return pltpu.make_async_remote_copy(
            src_ref=update.at[k, peers[j][0]], dst_ref=arrived.at[j, :, k * WIDTH : (k + 1) * WIDTH],
            send_sem=z_send.at[j, k], recv_sem=z_recv.at[j, k],
            device_id=(peers[j][0], r), device_id_type=MESH,
        )

    def map_to_peer(j):
        return pltpu.make_async_remote_copy(
            src_ref=slots.at[peers[j][0]], dst_ref=slots_in.at[j],
            send_sem=map_send.at[j], recv_sem=map_recv.at[j],
            device_id=(peers[j][0], r), device_id_type=MESH,
        )

    sent = []

    def start(copy):
        copy.start()
        sent.append(copy)

    def send_own(k):
        for t in range(len(direct)):
            start(ici(t, k))
        start(across_core(0, k, sources))

    def relay(k):
        for t in range(len(direct)):
            ici_in(t, k).wait_recv()
            if forward and t == 0:
                start(fwd(k))
            start(across_core(t + 1, k, sources))

    def keep(k):
        return pltpu.make_async_copy(
            update.at[k, c], arrived.at[len(peers), :, k * WIDTH : (k + 1) * WIDTH],
            keep_sem.at[k],
        )

    def part(k, source):
        at = pl.ds(pl.multiple_of(source * block, block), block)
        return dot(coupling[:, at], gathered[k, at, :])

    def last_arrivals(k):
        if forward:
            fwd_in(k).wait_recv()
            start(across_core(len(sources) - 1, k, sources))

    def multiply_as_it_comes(k):
        ready = sources[: len(direct) + 1]
        total[...] = part(k, ready[0])
        for source in ready[1:]:
            total[...] += part(k, source)
        for t in range(len(direct) + 1):
            across_core(t, k, other).wait_recv()
            total[...] += part(k, other[t])
        last_arrivals(k)
        if forward:
            total[...] += part(k, sources[-1])
            across_core(len(other) - 1, k, other).wait_recv()
            total[...] += part(k, other[-1])
        coupled[...] = total[...].astype(jnp.bfloat16)

    def multiply(k):
        last_arrivals(k)
        for t in range(len(sources)):
            across_core(t, k, other).wait_recv()
        depth = gathered.shape[1]
        piece = min(DEPTH, depth)
        value = dot(coupling[:, :piece], gathered[k, :piece, :])
        if depth > piece:
            def more(b, acc):
                at = pl.ds(pl.multiple_of(b * piece, piece), piece)
                return acc + dot(coupling[:, at], gathered[k, at, :])

            value = lax.fori_loop(1, depth // piece, more, value)
        coupled[...] = value.astype(jnp.bfloat16)

    def finish(k):
        for i in range(leaves):
            rows = slice(i * leaf, (i + 1) * leaf)
            value = local_part[rows, k * WIDTH : (k + 1) * WIDTH] + dot(
                u[rows, :], coupled[i * rank : (i + 1) * rank, :]
            )
            update[k, i] = value.astype(jnp.bfloat16)
        for j in range(len(peers)):
            start(to_peer(j, k))
        keep(k).start()

    loads[0].wait()
    loads[1].wait()
    project(0, 1)
    pl.semaphore_wait(barrier, len(direct) + 1 + len(peers))
    send_own(0)
    for j in range(len(peers)):
        start(map_to_peer(j))
    keep_slots = pltpu.make_async_copy(
        slots.at[c], slots_in.at[len(peers)], keep_sem.at[chunks]
    )
    keep_slots.start()
    loads[2].wait()
    if chunks > 1:
        project(1, chunks)
    for load in loads[3:]:
        load.wait()
    for i in range(leaves):
        rows = slice(i * leaf, (i + 1) * leaf)
        local_part[rows, :] = dot(diag[i], omega[rows, :])
    send_own(1)
    relay(0)
    send_own(2)
    for k in range(chunks):
        if k + 1 < chunks:
            relay(k + 1)
            if k + 3 < chunks:
                send_own(k + 3)
        if k in (0, chunks - 1):
            multiply_as_it_comes(k)
        else:
            multiply(k)
        finish(k)
    for j in range(len(peers)):
        map_to_peer(j).wait_recv()
    keep_slots.wait()
    for copy in sent:
        copy.wait_send()
    for k in range(chunks):
        keep(k).wait()
        for j in range(len(peers)):
            to_peer(j, k).wait_recv()


def combine(arrived, slots, out_ref):
    half = out_ref.shape[1]
    for j in range(arrived.shape[0]):
        value = arrived[j].astype(jnp.float32)
        low, high = value[:half], value[half:]
        s0, s1 = slots[j, 0:1, :], slots[j, 4:5, :]
        for q in range(3):
            term = jnp.where(s0 == float(q), low, jnp.where(s1 == float(q), high, 0.0))
            out_ref[q] = term if j == 0 else out_ref[q] + term


def solution(mesh):
    n_child, n_rows = mesh.shape["child"], mesh.shape["rows"]

    def on_device(omega, leaf_diag, leaf_u, leaf_v, coupling, child_map):
        leaves, leaf = leaf_diag.shape[1], leaf_diag.shape[2]
        rank, samples = leaf_u.shape[2], omega.shape[2]
        chunks = samples // WIDTH
        block, depth = coupling.shape[1], coupling.shape[2]
        chips = n_rows // 2
        direct = 2 if chips == 4 else chips - 1
        everyone = 1 + direct + (chips == 4)
        peers = n_child - 1
        vmem = pltpu.VMEM
        bf16, f32 = jnp.bfloat16, jnp.float32
        dma = pltpu.SemaphoreType.DMA
        anywhere = pl.BlockSpec(memory_space=pl.ANY)
        arrived, slots = pl.pallas_call(
            functools.partial(kernel, n_child, n_rows),
            out_shape=[
                jax.ShapeDtypeStruct((n_child, leaf, samples), bf16),
                jax.ShapeDtypeStruct((n_child, 8, samples), f32),
            ],
            in_specs=[anywhere] * 2 + [pl.BlockSpec(memory_space=pltpu.SMEM)] + [anywhere] * 3,
            out_specs=[anywhere] * 2,
            scratch_shapes=[
                vmem((leaves * leaf, samples), bf16),
                vmem((leaves * leaf, rank), bf16),
                vmem((leaves, leaf, leaf), bf16),
                vmem((leaves * leaf, rank), bf16),
                vmem((block, depth), bf16),
                vmem((chunks, depth, WIDTH), bf16),
                vmem((leaves * leaf, samples), f32),
                vmem((block, WIDTH), f32),
                vmem((block, WIDTH), bf16),
                vmem((chunks, leaves, leaf, WIDTH), bf16),
                vmem((leaves, 8, samples), f32),
                dma((6,)),
                dma((direct, chunks)),
                dma((direct, chunks)),
                dma((chunks,)),
                dma((chunks,)),
                dma((everyone, chunks)),
                dma((everyone, chunks)),
                dma((peers, chunks)),
                dma((peers, chunks)),
                dma((peers,)),
                dma((peers,)),
                dma((chunks + 1,)),
            ],
            compiler_params=pltpu.CompilerParams(
                collective_id=0, has_side_effects=True, vmem_limit_bytes=60000 * 1024
            ),
        )(omega, leaf_v, child_map, leaf_diag, leaf_u, coupling)
        width = samples // STEPS
        return pl.pallas_call(
            combine,
            grid=(STEPS,),
            out_shape=jax.ShapeDtypeStruct((3, leaf // 2, samples), f32),
            in_specs=[
                pl.BlockSpec((n_child, leaf, width), lambda i: (0, 0, i)),
                pl.BlockSpec((n_child, 8, width), lambda i: (0, 0, i)),
            ],
            out_specs=pl.BlockSpec((3, leaf // 2, width), lambda i: (0, 0, i)),
        )(arrived, slots)

    placed = (
        P("child", "rows", None),
        P("child", "rows", None, None),
        P("child", "rows", None),
        P("child", "rows", None),
        P("child", "rows", None),
        P("child", "rows"),
    )
    return jax.shard_map(
        on_device,
        mesh=mesh,
        in_specs=placed,
        out_specs=P(None, ("child", "rows"), None),
        check_vma=False,
    )
```

profile of v0, /device:TPU:0, one launch (start us, length us, event | category | flops | bytes accessed | tf_op | source)
XLA Modules:
  0.0 44.7 jit_solution(8111710571193732478)
XLA Ops:
  0.0 42.3 %shard_map.64 = (bf16[4,256,512]{2,1,0:T(8,128)(2,1)}, f32[4,8,512]{2,1,0:T(8,128)}) custom-call(bf16[1,1024,512]{2,1,0:T(8,128)(2,1)} %omega_hbm.1, bf16[1,1024,128]{2,1,0:T(8,128)(2,1)} %v_hbm.1, s32[1,8]{1,0:T(1,128)} %map_ref.1, bf16[1,4,256,256]{3,2,1,0:T(8,128)(2,1)} %diag_hbm.1, bf16[1,1024,128]{2,1,0:T(8,128)(2,1)} %u_hbm.1, ...), custom_call_target="tpu_custom_call" | custom-call | tf_op jit(solution)/shard_map/pallas_call | solution.py:298
  42.4 2.3 %shard_map.65 = f32[3,128,512]{2,1,0:T(8,128)} custom-call(bf16[4,256,512]{2,1,0:T(8,128)(2,1)} %get-tuple-element.7.arrived, f32[4,8,512]{2,1,0:T(8,128)} %get-tuple-element.8.slots), custom_call_target="tpu_custom_call" | custom-call | tf_op jit(solution)/shard_map/pallas_call | solution.py:336
where the time goes:
time: 44.8 us; the launch traced here: 44.7 us
  Pallas kernels  44.7 us (100%)
    pallas_call x1, Pallas kernels, on_device(): pl.pallas_call(functools.partial(kernel, n_child, n_rows), out_shape=[jax...  42.3 us
    pallas_call x1, Pallas kernels, on_device(): pl.pallas_call(combine, grid=(STEPS,), out_shape=jax.ShapeDtypeStruct((3,...  2.34 us

commit v1 on v0

v1 whole, which is shorter than its diff:
```python
import functools

import jax
import jax.numpy as jnp
from jax import lax
from jax.experimental import pallas as pl
from jax.experimental.pallas import tpu as pltpu
from jax.sharding import PartitionSpec as P

MESH = pl.DeviceIdType.MESH
WIDTH = 128
HALF = WIDTH // 2


def dot(a, b):
    return jnp.dot(a, b, preferred_element_type=jnp.float32)


def left_lanes(rows):
    return lax.broadcasted_iota(jnp.int32, (rows, WIDTH), 1) < HALF


def kernel(
    n_child, n_rows, omega_hbm, v_hbm, map_hbm, diag_hbm, u_hbm, coupling_hbm, out,
    omega, v, diag, u, coupling, gathered, local_part, total, coupled,
    halves, update, sums, halves_in, inner_in, near_in, far_in, maps, slots, slots_in, inner_slots,
    load_sem, ici_send, ici_recv, fwd_send, fwd_recv, core_send, core_recv,
    half_send, half_recv, inner_send, inner_recv, near_send, near_recv, far_send, far_recv,
    map_send, map_recv,
):
    groups, depth = gathered.shape[0], gathered.shape[1]
    leaves, leaf = diag.shape[0], diag.shape[1]
    rank = u.shape[1]
    block = leaves * rank
    chips = n_rows // 2
    last = groups
    c = lax.axis_index("child")
    r = lax.axis_index("rows")
    chip, core = r // 2, r % 2
    partner = chip * 2 + 1 - core

    forward = chips == 4
    if forward:
        x, y = chip % 2, chip // 2
        x_near = (y * 2 + 1 - x) * 2
        y_near = ((1 - y) * 2 + x) * 2
        first = x_near * (1 - core) + y_near * core
        second = y_near * (1 - core) + x_near * core
        across = ((1 - y) * 2 + 1 - x) * 2
        direct = [(second + core, second + core), (first + core, first + core)]
        other = [first + 1 - core, second + 1 - core]
    else:
        direct = [
            (((chip + d) % chips) * 2 + core, ((chip + chips - d) % chips) * 2 + core)
            for d in range(1, chips)
        ]
        other = [((chip + chips - d) % chips) * 2 + 1 - core for d in range(1, chips)]
    sources = [r] + [s for _, s in direct]
    other = [partner] + other
    if forward:
        sources.append(across + core)
        other.append(across + 1 - core)

    high = c // 2
    beside = c + 1 - 2 * (c % 2)
    peers = [3 - c, (c + 2) % 4, beside]
    is_inner = (c == 1) | (c == 2)
    is_outer = (c == 0) | (c == 3)
    ends = [3 - 3 * high, 2 - high]

    barrier = pltpu.get_barrier_semaphore()
    for to, _ in direct + [(partner, partner)]:
        pl.semaphore_signal(barrier, inc=1, device_id=(c, to), device_id_type=MESH)
    for to in peers:
        pl.semaphore_signal(barrier, inc=1, device_id=(to, r), device_id_type=MESH)

    loads = [
        pltpu.make_async_copy(v_hbm.at[0], v, load_sem.at[0]),
        pltpu.make_async_copy(
            omega_hbm.at[0, :, :WIDTH], omega.at[:, :WIDTH], load_sem.at[1]
        ),
        pltpu.make_async_copy(
            omega_hbm.at[0, :, WIDTH:], omega.at[:, WIDTH:], load_sem.at[2]
        ),
        pltpu.make_async_copy(map_hbm, maps, load_sem.at[3]),
        pltpu.make_async_copy(diag_hbm.at[0], diag, load_sem.at[4]),
        pltpu.make_async_copy(coupling_hbm.at[0], coupling, load_sem.at[5]),
        pltpu.make_async_copy(u_hbm.at[0], u, load_sem.at[6]),
    ]
    for load in loads:
        load.start()

    def packed(s):
        return s in (0, last)

    def piece(s, source):
        if packed(s):
            base = 0 if s == 0 else depth // 2
            size = block // 2
            return 0, pl.ds(pl.multiple_of(base + source * size, size), size)
        return s, pl.ds(pl.multiple_of(source * block, block), block)

    def rows_of(s, source):
        return gathered.at[piece(s, source)]

    def columns(g):
        return slice(g * WIDTH, (g + 1) * WIDTH)

    def project(i, cols):
        rows = slice(i * leaf, (i + 1) * leaf)
        return lax.dot_general(
            v[rows, :], omega[rows, cols], (((0,), (0,)), ((), ())),
            preferred_element_type=jnp.float32,
        )

    def project_first():
        mask = left_lanes(rank)
        for i in range(leaves // 2):
            low = project(i, columns(0))
            up = pltpu.roll(project(i + leaves // 2, columns(0)), HALF, 1)
            size = block // 2
            at = pl.multiple_of(r * size + i * rank, rank)
            gathered[0, pl.ds(at, rank), :] = jnp.where(mask, low, up).astype(jnp.bfloat16)
            at = pl.multiple_of(depth // 2 + r * size + i * rank, rank)
            gathered[0, pl.ds(at, rank), :] = jnp.where(mask, up, low).astype(jnp.bfloat16)

    def project_rest():
        for i in range(leaves):
            projected = project(i, slice(WIDTH, groups * WIDTH)).astype(jnp.bfloat16)
            at = pl.ds(pl.multiple_of(r * block + i * rank, rank), rank)
            for g in range(1, groups):
                gathered[g, at, :] = projected[:, (g - 1) * WIDTH : g * WIDTH]

    def remote(src, dst, send, recv, to):
        return pltpu.make_async_remote_copy(
            src_ref=src, dst_ref=dst, send_sem=send, recv_sem=recv,
            device_id=to, device_id_type=MESH,
        )

    def ici(t, s):
        at = rows_of(s, r)
        return remote(at, at, ici_send.at[t, s], ici_recv.at[t, s], (c, direct[t][0]))

    def ici_in(t, s):
        at = rows_of(s, direct[t][1])
        return remote(at, at, ici_send.at[t, s], ici_recv.at[t, s], (c, direct[t][0]))

    def fwd(s):
        at = rows_of(s, direct[0][1])
        return remote(at, at, fwd_send.at[s], fwd_recv.at[s], (c, direct[1][0]))

    def fwd_in(s):
        at = rows_of(s, sources[-1])
        return remote(at, at, fwd_send.at[s], fwd_recv.at[s], (c, direct[1][0]))

    def across_core(t, s, who):
        at = rows_of(s, who[t])
        return remote(at, at, core_send.at[t, s], core_recv.at[t, s], (c, partner))

    def half_to(j, h):
        return remote(
            halves.at[h, peers[j]], halves_in.at[h, j],
            half_send.at[h, j], half_recv.at[h, j], (peers[j], r),
        )

    def to_inner(e, g):
        return remote(
            update.at[g - 1, e], inner_in.at[g - 1, e],
            inner_send.at[g - 1, e], inner_recv.at[g - 1, e], (beside, r),
        )

    def to_near(g):
        return remote(
            update.at[g - 1, 2], near_in.at[g - 1],
            near_send.at[g - 1], near_recv.at[g - 1], (beside, r),
        )

    def to_far(e, g):
        return remote(
            sums.at[g - 1, e], far_in.at[g - 1],
            far_send.at[g - 1, e], far_recv.at[g - 1], (ends[e], r),
        )

    def map_to_peer(j):
        return remote(
            slots.at[peers[j]], slots_in.at[j], map_send.at[j], map_recv.at[j], (peers[j], r)
        )

    def map_to_inner(e):
        return remote(
            slots.at[ends[e]], inner_slots.at[e],
            map_send.at[3 + e], map_recv.at[3 + e], (beside, r),
        )

    sent = []

    def start(copy):
        copy.start()
        sent.append(copy)

    def send_own(t, s):
        if s <= last:
            start(ici(t, s))

    def send_core(s):
        if s <= last:
            start(across_core(0, s, sources))

    def arrive(t, s):
        if s <= last:
            ici_in(t, s).wait_recv()
            if forward and t == 0:
                start(fwd(s))
            start(across_core(t + 1, s, sources))

    def arrive_across(s):
        fwd_in(s).wait_recv()
        start(across_core(len(sources) - 1, s, sources))

    def part(s, source, fresh=False):
        k = s % 2
        if packed(s):
            g, at = piece(s, source)
            value = gathered[g, at, :]
            size = block // 2
            for h in range(2):
                cols = pl.ds(pl.multiple_of(source * block + h * size, size), size)
                term = dot(coupling[:, cols], value)
                total[k, h] = term if fresh else total[k, h] + term
        else:
            g, at = piece(s, source)
            term = dot(coupling[:, at], gathered[g, at, :])
            total[k, 0] = term if fresh else total[k, 0] + term

    def from_core(t, s):
        across_core(t, s, other).wait_recv()
        part(s, other[t])

    def settle(s):
        k = s % 2
        if packed(s):
            mask = left_lanes(block)
            a, b = (0, 1) if s == 0 else (1, 0)
            mixed = jnp.where(mask, total[k, a], total[k, b])
            coupled[k] = (mixed + pltpu.roll(mixed, HALF, 1)).astype(jnp.bfloat16)
        else:
            coupled[k] = total[k, 0].astype(jnp.bfloat16)

    def product(s, i):
        rows = pl.ds(pl.multiple_of(i * leaf, leaf), leaf)
        return dot(u[rows, :], coupled[s % 2, pl.ds(pl.multiple_of(i * rank, rank), rank), :])

    def local_rows(i):
        for g in range(groups):
            rows = slice(i * leaf, (i + 1) * leaf)
            value = dot(diag[i], omega[rows, columns(g)])
            if g == 0:
                mask = left_lanes(leaf // 2)
                low, up = value[: leaf // 2], pltpu.roll(value[leaf // 2 :], HALF, 1)
                local_part[i * leaf : i * leaf + leaf // 2, :WIDTH] = jnp.where(mask, low, up)
                local_part[i * leaf + leaf // 2 : (i + 1) * leaf, :WIDTH] = jnp.where(mask, up, low)
            else:
                local_part[rows, columns(g)] = value

    def finish_half(s):
        h = 0 if s == 0 else 1
        mask = left_lanes(leaf // 2)
        for j, i in enumerate(peers + [c]):
            value = product(s, i)
            low, up = value[: leaf // 2], value[leaf // 2 :]
            mixed = jnp.where(mask, low, up) if h == 0 else jnp.where(mask, up, low)
            rows = pl.ds(pl.multiple_of(i * leaf + h * (leaf // 2), leaf // 2), leaf // 2)
            halves[h, i] = (mixed + local_part[rows, :WIDTH]).astype(jnp.bfloat16)
            if j < len(peers):
                start(half_to(j, h))

    def finish_group(g):
        for e, i in enumerate(ends + [beside, c]):
            rows = pl.ds(pl.multiple_of(i * leaf, leaf), leaf)
            value = product(g, i) + local_part[rows, columns(g)]
            update[g - 1, e] = value.astype(jnp.bfloat16)
            if e < 2:
                @pl.when(is_outer)
                def _():
                    to_inner(e, g).start()
            elif e == 2:
                start(to_near(g))

    def finish(s):
        settle(s)
        if packed(s):
            finish_half(s)
        else:
            finish_group(s)

    def spread(low, up, slot, q):
        s0, s1 = slot[0:1, :], slot[4:5, :]
        return jnp.where(s0 == float(q), low, jnp.where(s1 == float(q), up, 0.0))

    def combine(g):
        if 1 <= g < last:
            @pl.when(is_inner)
            def _():
                for e in range(2):
                    to_inner(e, g).wait_recv()
                    own = update[g - 1, e].astype(jnp.float32)
                    got = inner_in[g - 1, e].astype(jnp.float32)
                    own_slot, got_slot = slots[ends[e]], inner_slots[e]
                    for q in range(3):
                        value = spread(
                            own[: leaf // 2], own[leaf // 2 :], own_slot, q
                        ) + spread(got[: leaf // 2], got[leaf // 2 :], got_slot, q)
                        sums[g - 1, e, q * (leaf // 2) : (q + 1) * (leaf // 2), :] = value.astype(
                            jnp.bfloat16
                        )
                    to_far(e, g).start()

    def final(g):
        if 1 <= g < last:
            to_near(g).wait_recv()
            to_far(0, g).wait_recv()
            own = update[g - 1, 3].astype(jnp.float32)
            got = near_in[g - 1].astype(jnp.float32)
            own_slot, got_slot = slots[c], slots_in[2]
            for q in range(3):
                far = far_in[g - 1, q * (leaf // 2) : (q + 1) * (leaf // 2), :]
                out[q, :, columns(g)] = (
                    spread(own[: leaf // 2], own[leaf // 2 :], own_slot, q)
                    + spread(got[: leaf // 2], got[leaf // 2 :], got_slot, q)
                    + far.astype(jnp.float32)
                )

    def final_halves():
        mask = left_lanes(leaf // 2)
        for j in [3, 2, 1, 0]:
            if j == 3:
                a, b, slot = halves[0, c], halves[1, c], slots[c]
            else:
                half_to(j, 1).wait_recv()
                a, b, slot = halves_in[0, j], halves_in[1, j], slots_in[j]
            a, b = a.astype(jnp.float32), b.astype(jnp.float32)
            low = jnp.where(mask, a, b)
            up = pltpu.roll(jnp.where(mask, b, a), HALF, 1)
            for q in range(3):
                term = spread(low, up, slot, q)
                out[q, :, :WIDTH] = term if j == 3 else out[q, :, :WIDTH] + term

    loads[0].wait()
    loads[1].wait()
    project_first()
    pl.semaphore_wait(barrier, len(direct) + 1 + len(peers))
    for t in reversed(range(len(direct))):
        send_own(t, 0)
    send_core(0)
    loads[2].wait()
    project_rest()
    send_own(0, 1)
    if not forward:
        for t in range(1, len(direct)):
            send_own(t, 1)
        send_core(1)
    loads[3].wait()
    for i in range(leaves):
        for b in range(2):
            slot = maps[0, 2 * i + b] - 3 * (r * leaves + i)
            slots[i, 4 * b : 4 * b + 4, :] = jnp.full((4, WIDTH), slot, jnp.int32).astype(
                jnp.float32
            )
    for j in range(len(peers)):
        start(map_to_peer(j))

    @pl.when(is_outer)
    def _():
        for e in range(2):
            map_to_inner(e).start()

    loads[4].wait()
    for i in range(leaves):
        local_rows(i)
    loads[5].wait()
    loads[6].wait()

    if forward:
        arrive(0, 0)
        send_own(1, 1)
        send_core(1)
        send_own(0, 2)
        arrive(1, 0)
        part(0, sources[0], True)
        part(0, sources[1])
        part(0, sources[2])
    for j in range(len(peers)):
        map_to_peer(j).wait_recv()

    @pl.when(is_inner)
    def _():
        for e in range(2):
            map_to_inner(e).wait_recv()

    for s in range(last + 1):
        if forward:
            arrive(0, s + 1)
            send_own(1, s + 2)
            send_core(s + 2)
            send_own(0, s + 3)
            from_core(0, s)
            arrive_across(s)
            from_core(1, s)
            from_core(2, s)
            part(s, sources[3])
            arrive(1, s + 1)
            if s < last:
                part(s + 1, sources[0], True)
                part(s + 1, sources[1])
            from_core(3, s)
            finish(s)
            if s < last:
                part(s + 1, sources[2])
        else:
            for t in range(len(direct)):
                arrive(t, s)
                send_own(t, s + 2)
            send_core(s + 2)
            for t in range(len(other)):
                across_core(t, s, other).wait_recv()
            part(s, 0, True)

            def more(i, carry, s=s):
                part(s, i)
                return carry

            lax.fori_loop(1, n_rows, more, 0)
            finish(s)
        combine(s - 1)
        final(s - 2)
    for g in range(max(1, last - 1), last):
        if g > last - 1:
            combine(g)
        final(g)
    for j in range(len(peers)):
        half_to(j, 0).wait_recv()
    final_halves()
    for copy in sent:
        copy.wait_send()

    @pl.when(is_outer)
    def _():
        for e in range(2):
            map_to_inner(e).wait_send()
            for g in range(1, last):
                to_inner(e, g).wait_send()

    @pl.when(is_inner)
    def _():
        for e in range(2):
            for g in range(1, last):
                to_far(e, g).wait_send()


def write(value, out, sem):
    copies = [
        pltpu.make_async_copy(value.at[q], out.at[q], sem.at[q]) for q in range(out.shape[0])
    ]
    for copy in copies:
        copy.start()
    for copy in copies:
        copy.wait()


def solution(mesh):
    n_child, n_rows = mesh.shape["child"], mesh.shape["rows"]

    def on_device(omega, leaf_diag, leaf_u, leaf_v, coupling, child_map):
        leaves, leaf = leaf_diag.shape[1], leaf_diag.shape[2]
        rank, samples = leaf_u.shape[2], omega.shape[2]
        groups = samples // WIDTH
        steps = groups + 1
        block, depth = coupling.shape[1], coupling.shape[2]
        chips = n_rows // 2
        direct = 2 if chips == 4 else chips - 1
        everyone = 1 + direct + (chips == 4)
        peers = n_child - 1
        vmem = pltpu.VMEM
        bf16, f32 = jnp.bfloat16, jnp.float32
        dma = pltpu.SemaphoreType.DMA
        anywhere = pl.BlockSpec(memory_space=pl.ANY)
        shape = (3, leaf // 2, samples)
        rest = groups - 1
        value = pl.pallas_call(
            functools.partial(kernel, n_child, n_rows),
            out_shape=vmem(shape, f32),
            in_specs=[anywhere] * 6,
            out_specs=pl.BlockSpec(memory_space=vmem),
            scratch_shapes=[
                vmem((leaves * leaf, samples), bf16),
                vmem((leaves * leaf, rank), bf16),
                vmem((leaves, leaf, leaf), bf16),
                vmem((leaves * leaf, rank), bf16),
                vmem((block, depth), bf16),
                vmem((groups, depth, WIDTH), bf16),
                vmem((leaves * leaf, samples), f32),
                vmem((2, 2, block, WIDTH), f32),
                vmem((2, block, WIDTH), bf16),
                vmem((2, leaves, leaf // 2, WIDTH), bf16),
                vmem((rest, 4, leaf, WIDTH), bf16),
                vmem((rest, 2, 3 * leaf // 2, WIDTH), bf16),
                vmem((2, peers, leaf // 2, WIDTH), bf16),
                vmem((rest, 2, leaf, WIDTH), bf16),
                vmem((rest, leaf, WIDTH), bf16),
                vmem((rest, 3 * leaf // 2, WIDTH), bf16),
                pltpu.SMEM(child_map.shape, jnp.int32),
                vmem((leaves, 8, WIDTH), f32),
                vmem((peers, 8, WIDTH), f32),
                vmem((2, 8, WIDTH), f32),
                dma((7,)),
                dma((direct, steps)),
                dma((direct, steps)),
                dma((steps,)),
                dma((steps,)),
                dma((everyone, steps)),
                dma((everyone, steps)),
                dma((2, peers)),
                dma((2, peers)),
                dma((rest, 2)),
                dma((rest, 2)),
                dma((rest,)),
                dma((rest,)),
                dma((rest, 2)),
                dma((rest,)),
                dma((peers + 2,)),
                dma((peers + 2,)),
            ],
            compiler_params=pltpu.CompilerParams(
                collective_id=0, has_side_effects=True, vmem_limit_bytes=52 * 1024 * 1024
            ),
        )(*[
            pltpu.with_memory_space_constraint(array, pltpu.HBM)
            for array in (omega, leaf_v, child_map, leaf_diag, leaf_u, coupling)
        ])
        value = pltpu.with_memory_space_constraint(value, vmem)
        return pl.pallas_call(
            write,
            out_shape=jax.ShapeDtypeStruct(shape, f32),
            in_specs=[pl.BlockSpec(memory_space=vmem)],
            out_specs=anywhere,
            scratch_shapes=[dma((3,))],
        )(value)

    placed = (
        P("child", "rows", None),
        P("child", "rows", None, None),
        P("child", "rows", None),
        P("child", "rows", None),
        P("child", "rows", None),
        P("child", "rows"),
    )
    return jax.shard_map(
        on_device,
        mesh=mesh,
        in_specs=placed,
        out_specs=P(None, ("child", "rows"), None),
        check_vma=False,
    )
```

time: 44.8 us -> 41.5 us (0.926)
  Pallas kernels: 44.7 us -> 41.4 us
    pallas_call x2, Pallas kernels: 44.7 us -> 41.4 us  [the longest x1 40.5 us: on_device(): pl.pallas_call(functools.partial(kernel, n_child, n_rows), out_shape=vmem...]
where the time goes in v1:
time: 41.5 us; the launch traced here: 41.4 us
  Pallas kernels  41.4 us (100%)
    pallas_call x1, Pallas kernels, on_device(): pl.pallas_call(functools.partial(kernel, n_child, n_rows), out_shape=vmem...  40.5 us
    pallas_call x1, Pallas kernels, on_device(): pl.pallas_call(write, out_shape=jax.ShapeDtypeStruct(shape, f32), in_spec...  0.9 us

profile of v1, /device:TPU:0, one launch (start us, length us, event | category | flops | bytes accessed | tf_op | source)
XLA Modules:
  0.0 41.4 jit_solution(17626085743422524304)
XLA Ops:
  0.0 40.5 %shard_map.64.value = f32[3,128,512]{2,1,0:T(8,128)S(1)} custom-call(bf16[1,1024,512]{2,1,0:T(8,128)(2,1)} %omega_hbm.1, bf16[1,1024,128]{2,1,0:T(8,128)(2,1)} %v_hbm.1, s32[1,8]{1,0:T(1,128)} %map_hbm.1, bf16[1,4,256,256]{3,2,1,0:T(8,128)(2,1)} %diag_hbm.1, bf16[1,1024,128]{2,1,0:T(8,128)(2,1)} %u_hbm.1, bf16[1,512,4096]{2,1,0:T(8,128)(2,1)} %coupling_hbm.1), custom_call_target="tpu_custom_call" | custom-call | tf_op jit(solution)/shard_map/pallas_call | solution.py:489
  40.5 0.9 %shard_map.65 = f32[3,128,512]{2,1,0:T(8,128)} custom-call(f32[3,128,512]{2,1,0:T(8,128)S(1)} %shard_map.64.value), custom_call_target="tpu_custom_call" | custom-call | tf_op jit(solution)/shard_map/pallas_call | solution.py:541

commit v2 on v1

v2 whole, which is shorter than its diff:
```python
import functools

import jax
import jax.numpy as jnp
from jax import lax
from jax.experimental import pallas as pl
from jax.experimental.pallas import tpu as pltpu
from jax.sharding import PartitionSpec as P

MESH = pl.DeviceIdType.MESH
WIDTH = 128
HALF = WIDTH // 2
AHEAD = 2
LAG = 2
DONE = 6


def dot(a, b):
    return jnp.dot(a, b, preferred_element_type=jnp.float32)


def left_lanes(rows):
    return lax.broadcasted_iota(jnp.int32, (rows, WIDTH), 1) < HALF


def kernel(
    n_child, n_rows, omega_hbm, v_hbm, map_hbm, diag_hbm, u_hbm, coupling_hbm, out,
    omega, v, diag, u, coupling, gathered, mine, near_total, local_part, total, coupled,
    update, sums, peer_in, inner_in, far_in, halves, maps, slots, slots_in, inner_slots,
    load_sem, ici_send, ici_recv, fwd_send, fwd_recv, core_send, core_recv, mine_send, mine_recv,
    peer_send, near_recv, peer_recv, inner_send, inner_recv, far_send, far_recv,
    map_send, map_recv, ready,
):
    groups, depth = gathered.shape[0], gathered.shape[1]
    leaves, leaf = diag.shape[0], diag.shape[1]
    rank = u.shape[1]
    block = leaves * rank
    chips = n_rows // 2
    steps = 2 * groups
    last = steps - 1
    c = lax.axis_index("child")
    r = lax.axis_index("rows")
    chip, core = r // 2, r % 2
    partner = chip * 2 + 1 - core

    forward = chips == 4
    if forward:
        x, y = chip % 2, chip // 2
        x_near = (y * 2 + 1 - x) * 2
        y_near = ((1 - y) * 2 + x) * 2
        first = x_near * (1 - core) + y_near * core
        second = y_near * (1 - core) + x_near * core
        across = ((1 - y) * 2 + 1 - x) * 2
        direct = [(second + core, second + core), (first + core, first + core)]
        other = [first + 1 - core, second + 1 - core]
    else:
        direct = [
            (((chip + d) % chips) * 2 + core, ((chip + chips - d) % chips) * 2 + core)
            for d in range(1, chips)
        ]
        other = [((chip + chips - d) % chips) * 2 + 1 - core for d in range(1, chips)]
    sources = [s for _, s in direct]
    if forward:
        sources.append(across + core)
        other.append(across + 1 - core)

    high = c // 2
    beside = c + 1 - 2 * (c % 2)
    peers = [3 - c, (c + 2) % 4, beside]
    is_inner = (c == 1) | (c == 2)
    is_outer = (c == 0) | (c == 3)
    ends = [3 - 3 * high, 2 - high]

    loads = [
        pltpu.make_async_copy(v_hbm.at[0], v, load_sem.at[0]),
        pltpu.make_async_copy(
            omega_hbm.at[0, :, :WIDTH], omega.at[:, :WIDTH], load_sem.at[1]
        ),
        pltpu.make_async_copy(
            omega_hbm.at[0, :, WIDTH:], omega.at[:, WIDTH:], load_sem.at[2]
        ),
        pltpu.make_async_copy(map_hbm, maps, load_sem.at[3]),
        pltpu.make_async_copy(diag_hbm.at[0], diag, load_sem.at[4]),
        pltpu.make_async_copy(coupling_hbm.at[0], coupling, load_sem.at[5]),
        pltpu.make_async_copy(u_hbm.at[0], u, load_sem.at[6]),
    ]
    for load in loads[:2]:
        load.start()

    barrier = pltpu.get_barrier_semaphore()
    for to, _ in direct + [(partner, partner)]:
        pl.semaphore_signal(barrier, inc=1, device_id=(c, to), device_id_type=MESH)
    pl.semaphore_signal(barrier, inc=1, device_id=(beside, r), device_id_type=MESH)

    @pl.when(is_inner)
    def _():
        pl.semaphore_signal(barrier, inc=1, device_id=(3 - c, r), device_id_type=MESH)

    through = (0, last)
    summed = steps - len(through)

    def direct_step(s):
        return s in through

    def piece(s, source):
        size = block // 2
        base = (s % 2) * (depth // 2)
        return s // 2, pl.ds(pl.multiple_of(base + source * size, size), size)

    def rows_of(s, source):
        return gathered.at[piece(s, source)]

    def columns(g):
        return slice(g * WIDTH, (g + 1) * WIDTH)

    def project(first, end):
        mask = left_lanes(rank)
        size = block // 2
        values = []
        for i in range(leaves):
            rows = slice(i * leaf, (i + 1) * leaf)
            values.append(
                lax.dot_general(
                    v[rows, :], omega[rows, first * WIDTH : end * WIDTH], (((0,), (0,)), ((), ())),
                    preferred_element_type=jnp.float32,
                )
            )
        for i in range(leaves):
            mine[0, i * rank : (i + 1) * rank, first * WIDTH : end * WIDTH] = values[i].astype(
                jnp.bfloat16
            )
        for i in range(leaves // 2):
            for g in range(first, end):
                cols = columns(g - first)
                low, up = values[i][:, cols], pltpu.roll(values[i + leaves // 2][:, cols], HALF, 1)
                at = pl.multiple_of(r * size + i * rank, rank)
                gathered[g, pl.ds(at, rank), :] = jnp.where(mask, low, up).astype(jnp.bfloat16)
                at = pl.multiple_of(depth // 2 + r * size + i * rank, rank)
                gathered[g, pl.ds(at, rank), :] = jnp.where(mask, up, low).astype(jnp.bfloat16)

    def remote(src, dst, send, recv, to):
        return pltpu.make_async_remote_copy(
            src_ref=src, dst_ref=dst, send_sem=send, recv_sem=recv,
            device_id=to, device_id_type=MESH,
        )

    def ici(t, s):
        at = rows_of(s, r)
        return remote(at, at, ici_send.at[t], ici_recv.at[t, s], (c, direct[t][0]))

    def ici_in(t, s):
        at = rows_of(s, direct[t][1])
        return remote(at, at, ici_send.at[t], ici_recv.at[t, s], (c, direct[t][0]))

    def fwd(s):
        at = rows_of(s, direct[0][1])
        return remote(at, at, fwd_send, fwd_recv.at[s], (c, direct[1][0]))

    def fwd_in(s):
        at = rows_of(s, sources[-1])
        return remote(at, at, fwd_send, fwd_recv.at[s], (c, direct[1][0]))

    def core_kind(t):
        return 1 if forward and t == 2 else 0

    def across_core(t, s, who):
        at = rows_of(s, who[t])
        return remote(at, at, core_send, core_recv.at[core_kind(t), s], (c, partner))

    def to_peer(j, s):
        return remote(
            update.at[s, peers[j]], peer_in.at[s, j],
            peer_send.at[j],
            near_recv.at[s] if j == 2 else peer_recv.at[through.index(s), j],
            (peers[j], r),
        )

    def to_inner(s):
        return remote(
            update.at[s, pl.ds(2 - 2 * high, 2)], inner_in.at[s],
            inner_send, inner_recv.at[s], (beside, r),
        )

    def to_far(e, s):
        return remote(
            sums.at[s, e], far_in.at[s], far_send, far_recv.at[s], (ends[e], r)
        )

    def to_partner():
        return remote(mine.at[0], mine.at[1], mine_send, mine_recv, (c, partner))

    def map_to_peer(j):
        return remote(
            slots.at[peers[j]], slots_in.at[j], map_send.at[0], map_recv.at[0], (peers[j], r)
        )

    def map_to_inner(e):
        return remote(
            slots.at[ends[e]], inner_slots.at[e],
            map_send.at[1], map_recv.at[1], (beside, r),
        )

    def from_partner(s, kind, count):
        at = gathered.at[0, pl.ds(0, count * (block // 2))]
        remote(at, at, core_send, core_recv.at[kind, s], (c, partner)).wait_recv()

    def start(copy):
        copy.start()

    def send_own(t, s):
        if s <= last:
            start(ici(t, s))

    def arrive(t, s):
        if s <= last:
            ici_in(t, s).wait_recv()
            if forward and t == 0:
                start(fwd(s))
            start(across_core(t, s, sources))

    def arrive_across(s):
        fwd_in(s).wait_recv()
        start(across_core(len(sources) - 1, s, sources))

    def part(s, source, fresh=False):
        k = s % 2
        g, at = piece(s, source)
        value = gathered[g, at, :]
        size = block // 2
        for h in range(2):
            cols = pl.ds(pl.multiple_of(source * block + h * size, size), size)
            term = dot(coupling[:, cols], value)
            total[k, h] = term if fresh else total[k, h] + term

    def settle(s):
        k = s % 2
        mask = left_lanes(block)
        known = near_total[:, columns(s // 2)]
        known = jnp.where(mask, known, 0.0) if k == 0 else jnp.where(mask, 0.0, known)
        mixed = jnp.where(mask, total[k, k], total[k, 1 - k]) + known
        coupled[k] = (mixed + pltpu.roll(mixed, HALF, 1)).astype(jnp.bfloat16)

    def local_rows(i):
        value = dot(diag[i], omega[i * leaf : (i + 1) * leaf, :])
        mask = left_lanes(leaf // 2)
        for g in range(groups):
            low = value[: leaf // 2, columns(g)]
            up = pltpu.roll(value[leaf // 2 :, columns(g)], HALF, 1)
            local_part[2 * g, i] = jnp.where(mask, low, up)
            local_part[2 * g + 1, i] = jnp.where(mask, up, low)

    def finish(s):
        settle(s)
        mask = left_lanes(leaf // 2)
        whole = direct_step(s)
        for e, i in enumerate((peers if whole else ends + [beside]) + [c]):
            rows = pl.ds(pl.multiple_of(i * leaf, leaf), leaf)
            at = pl.ds(pl.multiple_of(i * rank, rank), rank)
            value = dot(u[rows, :], coupled[s % 2, at, :])
            low, up = value[: leaf // 2], value[leaf // 2 :]
            mixed = jnp.where(mask, low, up) if s % 2 == 0 else jnp.where(mask, up, low)
            update[s, i] = (mixed + local_part[s, i]).astype(jnp.bfloat16)
            if whole and e < 3:
                start(to_peer(e, s))
            elif e == 1:
                @pl.when(is_outer)
                def _():
                    to_inner(s).start()
            elif e == 2:
                start(to_peer(2, s))

    def spread(value, slot, s):
        value = value.astype(jnp.float32)
        turned = pltpu.roll(value, HALF, 1)
        lanes = lax.broadcasted_iota(jnp.int32, (1, WIDTH), 1)
        main = lanes < HALF if s % 2 == 0 else lanes >= HALF
        s0, s1 = slot[0:1, :], slot[4:5, :]
        held, swapped = jnp.where(main, s0, s1), jnp.where(main, s1, s0)
        want = jnp.where(main, 0.0, 1.0)
        pair = jnp.where(held == want, value, jnp.where(swapped == want, turned, 0.0))
        third = jnp.where(held == 2.0, value, jnp.where(swapped == 2.0, turned, 0.0))
        quarter = leaf // 4
        mask = left_lanes(quarter)
        top, bottom = third[:quarter], third[quarter:]
        folded = jnp.where(mask, top, bottom) if s % 2 == 0 else jnp.where(mask, bottom, top)
        return jnp.concatenate([pair, folded], axis=0)

    def combine(s):
        if s >= 0 and not direct_step(s):
            @pl.when(is_inner)
            def _():
                to_inner(s).wait_recv()
                for e in range(2):
                    value = spread(update[s, ends[e]], slots[ends[e]], s) + spread(
                        inner_in[s, ends[e] - (2 - 2 * high)], inner_slots[e], s
                    )
                    sums[s, e] = value.astype(jnp.bfloat16)
                    to_far(e, s).start()

    def final(s):
        if s < 0:
            return
        value = spread(update[s, c], slots[c], s)
        if direct_step(s):
            for j in reversed(range(3)):
                to_peer(j, s).wait_recv()
                value = value + spread(peer_in[s, j], slots_in[j], s)
        else:
            to_peer(2, s).wait_recv()
            value = value + spread(peer_in[s, 2], slots_in[2], s)
            to_far(0, s).wait_recv()
            value = value + far_in[s].astype(jnp.float32)
        if s % 2 == 0:
            halves[...] = value
        else:
            cols, size, quarter = columns(s // 2), leaf // 2, leaf // 4
            mask = left_lanes(3 * quarter)
            before = halves[...]
            straight = jnp.where(mask, before, value)
            turned = pltpu.roll(jnp.where(mask, value, before), HALF, 1)
            out[0, :, cols] = straight[:size]
            out[1, :, cols] = turned[:size]
            out[2, :quarter, cols] = straight[size:]
            out[2, quarter:, cols] = turned[size:]

    loads[0].wait()
    loads[1].wait()
    for load in loads[2:]:
        load.start()
    project(0, 1)

    @pl.when(is_outer)
    def _():
        pl.semaphore_wait(barrier, len(direct) + 2)

    @pl.when(is_inner)
    def _():
        pl.semaphore_wait(barrier, len(direct) + 3)

    for t in reversed(range(len(direct))):
        send_own(t, 0)
    if forward:
        send_own(0, 1)
    loads[2].wait()
    project(1, groups)
    to_partner().start()
    for s in range(1, AHEAD):
        send_own(0, s + 1 if forward else s)
        if not forward:
            for t in range(1, len(direct)):
                send_own(t, s)

    def take_maps():
        remote(slots_in, slots_in, map_send.at[0], map_recv.at[0], (beside, r)).wait_recv()

        @pl.when(is_inner)
        def _():
            remote(
                inner_slots, inner_slots, map_send.at[1], map_recv.at[1], (beside, r)
            ).wait_recv()

    def take(s):
        arrive(0, s)
        send_own(1, s + 1)
        send_own(0, s + 1 + AHEAD)

    loads[3].wait()
    for i in range(leaves):
        for b in range(2):
            slot = maps[0, 2 * i + b] - 3 * (r * leaves + i)
            slots[i, 4 * b : 4 * b + 4, :] = jnp.full((4, WIDTH), slot, jnp.int32).astype(
                jnp.float32
            )

    @pl.when(is_inner)
    def _():
        pl.semaphore_signal(ready, inc=1, device_id=(3 - c, r), device_id_type=MESH)
        pl.semaphore_wait(ready, 1)
        pl.semaphore_signal(ready, inc=1, device_id=(beside, r), device_id_type=MESH)

    @pl.when(is_outer)
    def _():
        pl.semaphore_wait(ready, 1)

    for j in range(len(peers)):
        map_to_peer(j).start()

    @pl.when(is_outer)
    def _():
        for e in range(2):
            map_to_inner(e).start()

    if forward:
        take(0)
        arrive(1, 0)
        take(1)
    for load in loads[4:]:
        load.wait()
    for i in range(leaves):
        local_rows(i)
    near_total[...] = dot(coupling[:, pl.ds(pl.multiple_of(r * block, block), block)], mine[0])
    to_partner().wait_recv()
    near_total[...] += dot(
        coupling[:, pl.ds(pl.multiple_of(partner * block, block), block)], mine[1]
    )
    if forward:
        part(0, sources[0], True)
        part(0, sources[1])

    for s in range(steps):
        if forward:
            arrive_across(s)
            from_partner(s, 0, 2)
            for source in (other[0], other[1], sources[2]):
                part(s, source)
            if s + 2 <= last:
                take(s + 2)
            if s == 1:
                take_maps()
            combine(s - LAG)
            arrive(1, s + 1)
            if s < last:
                part(s + 1, sources[0], True)
                part(s + 1, sources[1])
            final(s - DONE)
            from_partner(s, 1, 1)
            part(s, other[2])
        else:
            for t in range(len(direct)):
                arrive(t, s)
                send_own(t, s + AHEAD)
            from_partner(s, 0, len(other))
            if s == 1:
                take_maps()
            combine(s - LAG)
            final(s - DONE)

            def more(d, carry, s=s):
                for e in range(2):
                    part(s, (chip + d) % chips * 2 + e)
                return carry

            part(s, (chip + 1) % chips * 2, True)
            part(s, (chip + 1) % chips * 2 + 1)
            lax.fori_loop(2, chips, more, 0)
        finish(s)
    for s in range(last - LAG + 1, steps):
        combine(s)
    for s in range(last - DONE + 1, steps):
        final(s)

    def drain(ref, sem):
        remote(ref, ref, sem, map_recv.at[0], (beside, r)).wait_send()

    for t in range(len(direct)):
        drain(gathered.at[:, pl.ds(0, block)], ici_send.at[t])
    if forward:
        drain(gathered.at[:, pl.ds(0, block)], fwd_send)
    drain(gathered.at[:, pl.ds(0, len(sources) * block)], core_send)
    to_partner().wait_send()
    for j in range(2):
        drain(update.at[0, pl.ds(0, len(through))], peer_send.at[j])
    drain(update.at[:, 0], peer_send.at[2])
    drain(slots.at[pl.ds(0, len(peers))], map_send.at[0])

    @pl.when(is_outer)
    def _():
        drain(slots.at[pl.ds(0, 2)], map_send.at[1])
        drain(update.at[pl.ds(0, summed), pl.ds(0, 2)], inner_send)

    @pl.when(is_inner)
    def _():
        drain(sums.at[pl.ds(0, summed)], far_send)


def write(value, out, sem):
    copies = [
        pltpu.make_async_copy(value.at[q], out.at[q], sem.at[q]) for q in range(out.shape[0])
    ]
    for copy in copies:
        copy.start()
    for copy in copies:
        copy.wait()


def solution(mesh):
    n_child, n_rows = mesh.shape["child"], mesh.shape["rows"]

    def on_device(omega, leaf_diag, leaf_u, leaf_v, coupling, child_map):
        leaves, leaf = leaf_diag.shape[1], leaf_diag.shape[2]
        rank, samples = leaf_u.shape[2], omega.shape[2]
        groups = samples // WIDTH
        steps = 2 * groups
        block, depth = coupling.shape[1], coupling.shape[2]
        chips = n_rows // 2
        direct = 2 if chips == 4 else chips - 1
        everyone = 1 + direct + (chips == 4)
        peers = n_child - 1
        vmem = pltpu.VMEM
        bf16, f32 = jnp.bfloat16, jnp.float32
        dma = pltpu.SemaphoreType.DMA
        anywhere = pl.BlockSpec(memory_space=pl.ANY)
        shape = (3, leaf // 2, samples)
        value = pl.pallas_call(
            functools.partial(kernel, n_child, n_rows),
            out_shape=vmem(shape, f32),
            in_specs=[anywhere] * 6,
            out_specs=pl.BlockSpec(memory_space=vmem),
            scratch_shapes=[
                vmem((leaves * leaf, samples), bf16),
                vmem((leaves * leaf, rank), bf16),
                vmem((leaves, leaf, leaf), bf16),
                vmem((leaves * leaf, rank), bf16),
                vmem((block, depth), bf16),
                vmem((groups, depth, WIDTH), bf16),
                vmem((2, block, samples), bf16),
                vmem((block, samples), f32),
                vmem((steps, leaves, leaf // 2, WIDTH), f32),
                vmem((2, 2, block, WIDTH), f32),
                vmem((2, block, WIDTH), bf16),
                vmem((steps, leaves, leaf // 2, WIDTH), bf16),
                vmem((steps, 2, 3 * leaf // 4, WIDTH), bf16),
                vmem((steps, peers, leaf // 2, WIDTH), bf16),
                vmem((steps, 2, leaf // 2, WIDTH), bf16),
                vmem((steps, 3 * leaf // 4, WIDTH), bf16),
                vmem((3 * leaf // 4, WIDTH), f32),
                pltpu.SMEM(child_map.shape, jnp.int32),
                vmem((leaves, 8, WIDTH), f32),
                vmem((peers, 8, WIDTH), f32),
                vmem((2, 8, WIDTH), f32),
                dma((7,)),
                dma((direct,)),
                dma((direct, steps)),
                dma,
                dma((steps,)),
                dma,
                dma((2, steps)),
                dma,
                dma,
                dma((peers,)),
                dma((steps,)),
                dma((2, 2)),
                dma,
                dma((steps,)),
                dma,
                dma((steps,)),
                dma((2,)),
                dma((2,)),
                pltpu.SemaphoreType.REGULAR,
            ],
            compiler_params=pltpu.CompilerParams(
                collective_id=0, has_side_effects=True, vmem_limit_bytes=52 * 1024 * 1024
            ),
        )(*[
            pltpu.with_memory_space_constraint(array, pltpu.HBM)
            for array in (omega, leaf_v, child_map, leaf_diag, leaf_u, coupling)
        ])
        value = pltpu.with_memory_space_constraint(value, vmem)
        return pl.pallas_call(
            write,
            out_shape=jax.ShapeDtypeStruct(shape, f32),
            in_specs=[pl.BlockSpec(memory_space=vmem)],
            out_specs=anywhere,
            scratch_shapes=[dma((3,))],
        )(value)

    placed = (
        P("child", "rows", None),
        P("child", "rows", None, None),
        P("child", "rows", None),
        P("child", "rows", None),
        P("child", "rows", None),
        P("child", "rows"),
    )
    return jax.shard_map(
        on_device,
        mesh=mesh,
        in_specs=placed,
        out_specs=P(None, ("child", "rows"), None),
        check_vma=False,
    )
```

time: 41.5 us -> 39 us (0.940)
  Pallas kernels: 41.4 us -> 38.8 us
    pallas_call x1, Pallas kernels: 40.5 us -> 37.9 us  [on_device(): pl.pallas_call(functools.partial(kernel, n_child, n_rows), out_shape=vmem...]
where the time goes in v2:
time: 39 us; the launch traced here: 38.9 us
  Pallas kernels  38.8 us (99%)
    pallas_call x1, Pallas kernels, on_device(): pl.pallas_call(functools.partial(kernel, n_child, n_rows), out_shape=vmem...  37.9 us
    pallas_call x1, Pallas kernels, on_device(): pl.pallas_call(write, out_shape=jax.ShapeDtypeStruct(shape, f32), in_spec...  0.9 us

profile of v2, /device:TPU:0, one launch (start us, length us, event | category | flops | bytes accessed | tf_op | source)
XLA Modules:
  0.0 38.9 jit_solution(6699097922824385976)
XLA Ops:
  0.0 37.9 %shard_map.64.value = f32[3,128,512]{2,1,0:T(8,128)S(1)} custom-call(bf16[1,1024,512]{2,1,0:T(8,128)(2,1)} %omega_hbm.1, bf16[1,1024,128]{2,1,0:T(8,128)(2,1)} %v_hbm.1, s32[1,8]{1,0:T(1,128)} %map_hbm.1, bf16[1,4,256,256]{3,2,1,0:T(8,128)(2,1)} %diag_hbm.1, bf16[1,1024,128]{2,1,0:T(8,128)(2,1)} %u_hbm.1, bf16[1,512,4096]{2,1,0:T(8,128)(2,1)} %coupling_hbm.1), custom_call_target="tpu_custom_call" | custom-call | tf_op jit(solution)/shard_map/pallas_call | solution.py:504
  38.0 0.9 %shard_map.65 = f32[3,128,512]{2,1,0:T(8,128)} custom-call(f32[3,128,512]{2,1,0:T(8,128)S(1)} %shard_map.64.value), custom_call_target="tpu_custom_call" | custom-call | tf_op jit(solution)/shard_map/pallas_call | solution.py:559

commit v3 on v2

--- a/solution.py
+++ b/solution.py
@@ -13,6 +13,7 @@
 AHEAD = 2
 LAG = 2
 DONE = 6
+LATE = 2
 
 
 def dot(a, b):
@@ -96,7 +97,7 @@
     def _():
         pl.semaphore_signal(barrier, inc=1, device_id=(3 - c, r), device_id_type=MESH)
 
-    through = (0, last)
+    through = (0,)
     summed = steps - len(through)
 
     def direct_step(s):
@@ -249,6 +250,10 @@
             local_part[2 * g, i] = jnp.where(mask, low, up)
             local_part[2 * g + 1, i] = jnp.where(mask, up, low)
 
+    def near_later(s):
+        if s >= 0 and not direct_step(s):
+            start(to_peer(2, s))
+
     def finish(s):
         settle(s)
         mask = left_lanes(leaf // 2)
@@ -267,7 +272,7 @@
                 def _():
                     to_inner(s).start()
             elif e == 2:
-                start(to_peer(2, s))
+                near_later(s - LATE)
 
     def spread(value, slot, s):
         value = value.astype(jnp.float32)
@@ -444,9 +449,14 @@
             part(s, (chip + 1) % chips * 2 + 1)
             lax.fori_loop(2, chips, more, 0)
         finish(s)
-    for s in range(last - LAG + 1, steps):
+    for s in range(last - LATE + 1, steps):
+        near_later(s)
+    for s in range(last - LAG + 1, last):
         combine(s)
-    for s in range(last - DONE + 1, steps):
+    for s in range(last - DONE + 1, last - 2):
+        final(s)
+    combine(last)
+    for s in range(last - 2, steps):
         final(s)
 
     def drain(ref, sem):
@@ -459,7 +469,7 @@
     drain(gathered.at[:, pl.ds(0, len(sources) * block)], core_send)
     to_partner().wait_send()
     for j in range(2):
-        drain(update.at[0, pl.ds(0, len(through))], peer_send.at[j])
+        drain(gathered.at[0, pl.ds(0, 128*len(through))], peer_send.at[j])
     drain(update.at[:, 0], peer_send.at[2])
     drain(slots.at[pl.ds(0, len(peers))], map_send.at[0])
 
@@ -539,7 +549,7 @@
                 dma,
                 dma((peers,)),
                 dma((steps,)),
-                dma((2, 2)),
+                dma((8, 2)),
                 dma,
                 dma((steps,)),
                 dma,

time: 39 us -> 37.8 us (0.969)
  Pallas kernels: 38.8 us -> 37.7 us
    pallas_call x1, Pallas kernels: 37.9 us -> 36.8 us  [on_device(): pl.pallas_call(functools.partial(kernel, n_child, n_rows), out_shape=vmem...]
where the time goes in v3:
time: 37.8 us; the launch traced here: 37.7 us
  Pallas kernels  37.7 us (100%)
    pallas_call x1, Pallas kernels, on_device(): pl.pallas_call(functools.partial(kernel, n_child, n_rows), out_shape=vmem...  36.8 us
    pallas_call x1, Pallas kernels, on_device(): pl.pallas_call(write, out_shape=jax.ShapeDtypeStruct(shape, f32), in_spec...  0.9 us

profile of v3, /device:TPU:0, one launch (start us, length us, event | category | flops | bytes accessed | tf_op | source)
XLA Modules:
  0.0 37.7 jit_solution(16499562803227335198)
XLA Ops:
  0.0 36.8 %shard_map.64.value = f32[3,128,512]{2,1,0:T(8,128)S(1)} custom-call(bf16[1,1024,512]{2,1,0:T(8,128)(2,1)} %omega_hbm.1, bf16[1,1024,128]{2,1,0:T(8,128)(2,1)} %v_hbm.1, s32[1,8]{1,0:T(1,128)} %map_hbm.1, bf16[1,4,256,256]{3,2,1,0:T(8,128)(2,1)} %diag_hbm.1, bf16[1,1024,128]{2,1,0:T(8,128)(2,1)} %u_hbm.1, bf16[1,512,4096]{2,1,0:T(8,128)(2,1)} %coupling_hbm.1), custom_call_target="tpu_custom_call" | custom-call | tf_op jit(solution)/shard_map/pallas_call | solution.py:514
  36.8 0.9 %shard_map.65 = f32[3,128,512]{2,1,0:T(8,128)} custom-call(f32[3,128,512]{2,1,0:T(8,128)S(1)} %shard_map.64.value), custom_call_target="tpu_custom_call" | custom-call | tf_op jit(solution)/shard_map/pallas_call | solution.py:569

commit v4 on v3

--- a/solution.py
+++ b/solution.py
@@ -346,6 +346,11 @@
         send_own(t, 0)
     if forward:
         send_own(0, 1)
+
+    @pl.when(is_inner)
+    def _():
+        pl.semaphore_signal(ready, inc=1, device_id=(3 - c, r), device_id_type=MESH)
+
     loads[2].wait()
     project(1, groups)
     to_partner().start()
@@ -379,7 +384,6 @@
 
     @pl.when(is_inner)
     def _():
-        pl.semaphore_signal(ready, inc=1, device_id=(3 - c, r), device_id_type=MESH)
         pl.semaphore_wait(ready, 1)
         pl.semaphore_signal(ready, inc=1, device_id=(beside, r), device_id_type=MESH)
 

time: 37.8 us -> 37.8 us (level)
  no operation moved by 1% of the time
where the time goes in v4:
time: 37.8 us; the launch traced here: 37.7 us
  Pallas kernels  37.7 us (100%)
    pallas_call x1, Pallas kernels, on_device(): pl.pallas_call(functools.partial(kernel, n_child, n_rows), out_shape=vmem...  36.8 us
    pallas_call x1, Pallas kernels, on_device(): pl.pallas_call(write, out_shape=jax.ShapeDtypeStruct(shape, f32), in_spec...  0.9 us

profile of v4, /device:TPU:0, one launch (start us, length us, event | category | flops | bytes accessed | tf_op | source)
XLA Modules:
  0.0 37.7 jit_solution(16979497399535074972)
XLA Ops:
  0.0 36.8 %shard_map.64.value = f32[3,128,512]{2,1,0:T(8,128)S(1)} custom-call(bf16[1,1024,512]{2,1,0:T(8,128)(2,1)} %omega_hbm.1, bf16[1,1024,128]{2,1,0:T(8,128)(2,1)} %v_hbm.1, s32[1,8]{1,0:T(1,128)} %map_hbm.1, bf16[1,4,256,256]{3,2,1,0:T(8,128)(2,1)} %diag_hbm.1, bf16[1,1024,128]{2,1,0:T(8,128)(2,1)} %u_hbm.1, bf16[1,512,4096]{2,1,0:T(8,128)(2,1)} %coupling_hbm.1), custom_call_target="tpu_custom_call" | custom-call | tf_op jit(solution)/shard_map/pallas_call | solution.py:518
  36.8 0.9 %shard_map.65 = f32[3,128,512]{2,1,0:T(8,128)} custom-call(f32[3,128,512]{2,1,0:T(8,128)S(1)} %shard_map.64.value), custom_call_target="tpu_custom_call" | custom-call | tf_op jit(solution)/shard_map/pallas_call | solution.py:573
